TPU v7x, 32 devices: a whole 2x2x4 slice. The times are simulated.
32 devices in a mesh: grp: 4 (over x, core), row: 4 (over z), col: 2 (over y).
Axes of the slice: x: 2, y: 2, z: 4, core: 2. Of those that a mesh axis runs over, the one named last changes fastest.
Arguments:
- fields: bfloat16 [4, 4, 192, 1536], P('grp', None, 'row', 'col'), may hold values from -12 to 12
- offset: int32 [1], replicated, may hold values from 0 to 191
- level_index: int32 [4], replicated, may hold values from 0 to 3, each once
- nudge_rate: float32 [4], replicated, may hold values from 0.2 to 0.9
- driving: float32 [4, 64, 64], replicated, may hold values from -4 to 4
Outputs:
- nudged: bfloat16 [4, 4, 192, 1536], P('grp', None, 'row', 'col')
Inputs may be any that keep to these rules, and one draw needn't show every extreme that they name: `offset`: the footprint covers a third of the parent rows from there on, wrapping around the periodic domain. `level_index`: each parent level is fed by exactly one child level.
All inputs are finite; a program needn't handle non-finite values.
Results may differ from a plain program's by a relative error of at most 0.0034.
Values may be sent and summed in bfloat16 or wider, within the bound.
No kernel may reach another device: no remote copies, remote signals or barrier semaphores. Data moves between devices by JAX's collectives and lax.ppermute only.
A program may use at most 64 MiB of HBM per device.

v0:
```python
import math
import jax
import jax.numpy as jnp
from jax import lax
from jax.sharding import PartitionSpec as P

MAX_WAVE = 32


def from_root(block, axis, source):
    block = jnp.where(lax.axis_index(axis) == source, block, jnp.zeros_like(block))
    return lax.psum(block, axis)


def fourier_table(positions, cell_count, max_order):
    orders = jnp.arange(1, max_order + 1, dtype=jnp.int32)
    period = 3 * cell_count
    phase_index = positions[:, None] * orders[None, :] % period
    angles = phase_index.astype(jnp.float32) * jnp.float32(2.0 * math.pi / period)
    wave_scale = jnp.float32(math.sqrt(2.0 / cell_count))
    constant = jnp.full((positions.shape[0], 1), 1.0 / math.sqrt(cell_count), jnp.float32)
    return jnp.concatenate(
        [constant, wave_scale * jnp.cos(angles), wave_scale * jnp.sin(angles[:, : max_order - 1])],
        axis=1,
    )


def place_rows(carried, block_rows, strip_index):
    height = block_rows.shape[1]
    inside = (strip_index >= 0) & (strip_index < height)
    picked = jnp.take(block_rows, jnp.clip(strip_index, 0, height - 1), axis=1)
    mask_shape = (1, inside.shape[0]) + (1,) * (block_rows.ndim - 2)
    return jnp.where(inside.reshape(mask_shape), picked, carried)


def per_device(fields, offset, level_index, nudge_rate, driving):
    group_id = lax.axis_index("grp")
    row_id = lax.axis_index("row")
    col_id = lax.axis_index("col")
    group_count = lax.axis_size("grp")
    local_slab = fields[0]
    levels, tile_rows, tile_cols = local_slab.shape
    full_rows = lax.axis_size("row") * tile_rows
    full_cols = lax.axis_size("col") * tile_cols
    third_rows = tile_rows // 3
    third_cols = tile_cols // 3
    shift_rows = offset[0]
    is_parent = group_id == group_count - 1
    level_ids = jnp.arange(levels, dtype=jnp.int32)
    inverse = jnp.sum(
        level_ids[:, None] * (level_index[:, None] == level_ids[None, :]).astype(jnp.int32), axis=0
    )
    parent_rows = row_id * tile_rows + jnp.arange(tile_rows, dtype=jnp.int32)
    parent_cols = col_id * tile_cols + jnp.arange(tile_cols, dtype=jnp.int32)
    strip_index = (parent_rows - shift_rows) % full_rows
    covered = strip_index < full_rows // 3
    row_table = fourier_table(3 * parent_rows, full_rows, MAX_WAVE)
    col_table = fourier_table(3 * parent_cols, full_cols, MAX_WAVE)
    row_half = lax.optimization_barrier(row_table.astype(jnp.bfloat16))
    row_rounded = row_half.astype(jnp.float32)
    col_rounded = col_table.astype(jnp.bfloat16)
    block_sums = jnp.sum(
        local_slab.reshape(levels, third_rows, 3, third_cols, 3), axis=(2, 4), dtype=jnp.float32
    )
    averaged = (block_sums / 9.0).astype(jnp.bfloat16)
    by_parent = jnp.take(averaged, inverse, axis=0)
    empty_tile = jnp.zeros((levels, tile_rows, third_cols), jnp.bfloat16)
    placed = place_rows(
        empty_tile, lax.all_gather(by_parent, "row", axis=1, tiled=True), strip_index
    )
    thirds = lax.all_gather(placed[:, :, None, :], "grp", axis=2, tiled=True)
    arrived = thirds[:, :, : group_count - 1, :].reshape(levels, tile_rows, tile_cols)
    fed_tile = jnp.where(covered[None, :, None], arrived, local_slab)
    projected = jnp.einsum("lrc,cm->lrm", fed_tile, col_rounded, preferred_element_type=jnp.float32)
    partial_sums = jnp.einsum(
        "rn,lrm->lnm", row_rounded, projected, precision=lax.Precision.HIGHEST
    )
    summed = lax.psum(partial_sums, ("row", "col"))
    coeffs = from_root(summed, "grp", group_count - 1)
    amplitude = math.sqrt(full_rows * full_cols) / (2 * MAX_WAVE)
    deficit = amplitude * driving - coeffs
    child_rows = (3 * shift_rows + parent_rows - 1) % (3 * full_rows)
    child_cols = (
        (3 * col_id + group_id) * tile_cols + jnp.arange(tile_cols, dtype=jnp.int32) - 1
    ) % (3 * full_cols)
    rows_used = jnp.where(is_parent, row_table, fourier_table(child_rows, full_rows, MAX_WAVE))
    cols_used = jnp.where(is_parent, col_table, fourier_table(child_cols, full_cols, MAX_WAVE))
    level_deficit = jnp.where(is_parent, deficit, jnp.take(deficit, level_index, axis=0))
    level_rate = jnp.where(is_parent, nudge_rate, jnp.take(nudge_rate, level_index, axis=0))
    base_tile = jnp.where(is_parent, fed_tile, local_slab)
    spread_cols = jnp.einsum(
        "lnm,cm->lnc", level_deficit, cols_used, precision=lax.Precision.HIGHEST
    )
    increment = jnp.einsum("rn,lnc->lrc", rows_used, spread_cols, precision=lax.Precision.HIGHEST)
    result = (base_tile.astype(jnp.float32) + level_rate[:, None, None] * increment).astype(
        jnp.bfloat16
    )
    return result[None]


def solution(mesh):
    placed = (P("grp", None, "row", "col"), P(), P(), P(), P())
    return jax.shard_map(
        per_device,
        mesh=mesh,
        in_specs=placed,
        out_specs=P("grp", None, "row", "col"),
        check_vma=False,
    )
```

profile of v0, /device:TPU:0, one launch (start us, length us, event | category | flops | bytes accessed | tf_op | source)
XLA Modules:
  0.0 187.4 jit_solution(7154075441931077724)
XLA Ops:
  6.5 0.7 select_reduce_fusion
  8.0 0.0 copy-start.1
  8.1 25.9 %reshape.136 = f32[4,16,3,256,3]{4,3,2,1,0:T(8,128)} reshape(bf16[1,4,48,768]{3,2,1,0:T(8,128)(2,1)} %param.5) | data formatting | bytes 884736 | tf_op jit(solution)/shard_map/convert_element_type | solution.py:62
  34.0 11.8 %reduce_sum.21 = f32[4,16,256]{2,1,0:T(8,128)S(1)} reduce(f32[4,16,3,256,3]{4,3,2,1,0:T(8,128)} %reshape.136, f32[]{:T(128)} %constant.140.clone.1), dimensions={2,4}, to_apply=%region_1.2 | reduce | flops 131072 | bytes 655364 | tf_op jit(solution)/shard_map/reduce_sum | solution.py:62
  45.8 0.5 gather_fusion
  46.3 0.1 broadcast_select_fusion.1
  46.4 15.1 %all_gather.6 = bf16[4,64,256]{2,1,0:T(8,128)(2,1)S(1)} all-gather(bf16[4,16,256]{2,1,0:T(8,128)(2,1)S(1)} %broadcast_select_fusion.1), channel_id=1, replica_groups=mesh['grp'=4,'row'=4,'col'=2] {'row'}, dimensions={1}, use_global_device_ids=true | all-gather | bytes 163840 | tf_op jit(solution)/shard_map/all_gather | solution.py:69
  61.5 0.1 copy.20
  61.6 0.7 gather_fusion.1
  62.3 0.1 fusion.24
  62.4 6.5 %all_gather.7 = bf16[4,48,4,256]{3,1,0,2:T(8,128)(2,1)S(1)} all-gather(bf16[4,48,1,256]{3,1,0,2:T(8,128)(2,1)S(1)} %fusion.24), channel_id=1, replica_groups=mesh['grp'=4,'row'=4,'col'=2] {'grp'}, dimensions={2}, use_global_device_ids=true | all-gather | bytes 491520 | tf_op jit(solution)/shard_map/all_gather | solution.py:71
  68.9 0.8 cosine_multiply_fusion.1
  69.7 0.3 fusion.21
  70.1 0.3 cosine_multiply_fusion.2
  70.4 0.1 fusion.40
  70.5 0.1 fusion.55
  70.6 0.3 fusion.13
  70.9 1.0 convolution_bitcast_fusion
  71.9 0.0 all-reduce.3.cloned.1.call-update
  71.9 0.0 all-reduce.5.cloned.1.call-start
  72.0 0.3 fusion.20
  72.3 0.1 fusion.39
  72.4 0.6 gather_fusion.2
  73.1 70.4 %all-reduce.3.cloned.1.call-done = f32[4,64,64]{1,2,0:T(8,128)} async-done(((f32[4,64,64]{1,2,0:T(8,128)}), f32[4,64,64]{1,2,0:T(8,128)}) %all-reduce.3.cloned.1.call-update) | async-done | bytes 65552 | tf_op jit(solution)/shard_map/psum | solution.py:78
  143.4 0.7 broadcast_select_fusion
  144.1 0.0 all-reduce.5.cloned.1.call-update
  144.1 0.1 copy.23
  144.2 32.4 %all-reduce.5.cloned.1.call-done = f32[4,64,64]{1,2,0:T(8,128)} async-done(((f32[4,64,64]{1,2,0:T(8,128)}), f32[4,64,64]{1,2,0:T(8,128)}) %all-reduce.5.cloned.1.call-update) | async-done | bytes 65552 | tf_op jit(solution)/shard_map/psum | solution.py:12
  176.6 0.9 multiply_subtract_fusion
  177.6 0.6 gather_fusion.3
  178.1 0.9 fusion.5
  179.1 1.5 fusion.3
  (27 shorter events, 0.2 us)
Async XLA Ops:
  6.5 136.9 %all-reduce.3.cloned.1.call-start = ((), (), s32[]{:S(2)}) async-start(), calls=%async_computation | async-start | bytes 262144 | tf_op jit(solution)/shard_map/psum | solution.py:78
  8.0 62.6 %copy-start.1 = (bf16[1,4,48,768]{3,2,1,0:T(8,128)(2,1)S(1)}, bf16[1,4,48,768]{3,2,1,0:T(8,128)(2,1)}, u32[]{:S(2)}) copy-start(bf16[1,4,48,768]{3,2,1,0:T(8,128)(2,1)} %param.5) | copy-start | bytes 884740
  8.0 63.9 %copy-start.3 = (s32[4]{0:T(128)S(1)}, s32[4]{0:T(128)}, u32[]{:S(2)}) copy-start(s32[4]{0:T(128)} %param.7) | copy-start | bytes 52
  8.0 64.4 %copy-start = (f32[4]{0:T(128)S(1)}, f32[4]{0:T(128)}, u32[]{:S(2)}) copy-start(f32[4]{0:T(128)} %param.8) | copy-start | bytes 52
  8.0 136.1 %copy-start.2 = (f32[4,64,64]{2,1,0:T(8,128)S(1)}, f32[4,64,64]{2,1,0:T(8,128)}, u32[]{:S(2)}) copy-start(f32[4,64,64]{2,1,0:T(8,128)} %param.9) | copy-start | bytes 196612
  71.9 104.8 %all-reduce.5.cloned.1.call-start = ((), (), s32[]{:S(2)}) async-start(), calls=%async_computation.1 | async-start | bytes 262144 | tf_op jit(solution)/shard_map/psum | solution.py:12
Sparse Core Ops, SparseCore 0:
  72.0 71.3 all-reduce.2
  145.7 30.8 all-reduce.4
where the time goes:
time: 188 us; the launch traced here: 187 us
  waiting for transfers between devices  103 us (55%)
  local copies, waits for them, and re-layouts  28.6 us (15%)
  blocking collectives  21.5 us (11%)
  other arithmetic  16.5 us (9%)
  between operations  14.3 us (8%)
  matrix products  3.65 us (2%)
    psum x1, waiting for transfers between devices, per_device(): summed = lax.psum(partial_sums, ('row', 'col'))  70.4 us
    psum x1, waiting for transfers between devices, from_root(): return lax.psum(block, axis)  32.4 us
    convert_element_type x1, local copies, waits for them, and re-layouts, per_device(): jnp.sum(local_slab.reshape(levels, third_rows, 3, third_cols, 3), axis=(2...  25.9 us
    all_gather x1, blocking collectives, per_device(): lax.all_gather(by_parent, 'row', axis=1, tiled=True)  15.1 us
    reduce_sum x1, other arithmetic, per_device(): jnp.sum(local_slab.reshape(levels, third_rows, 3, third_cols, 3), axis=(2...  11.8 us
    all_gather x1, blocking collectives, per_device(): thirds = lax.all_gather(placed[:, :, None, :], 'grp', axis=2, tiled=True)  6.46 us
  transfers between devices with their start and end apart: 2, of which 2 were waited for; matrix products, arithmetic and copies ran while one was open for 1% of the time, Pallas kernels for 0%

commit v1 on v0

--- a/solution.py
+++ b/solution.py
@@ -9,7 +9,7 @@
 
 def from_root(block, axis, source):
     block = jnp.where(lax.axis_index(axis) == source, block, jnp.zeros_like(block))
-    return lax.psum(block, axis)
+    return jnp.sum(lax.all_gather(block, axis), axis=0)
 
 
 def fourier_table(positions, cell_count, max_order):

time: 188 us -> 161 us (0.86)
  waiting for transfers between devices: 103 us -> 70.3 us
  blocking collectives: 21.5 us -> 28.7 us
    psum x1 -> x0, waiting for transfers between devices: 32.4 us -> none  [from_root(): return lax.psum(block, axis)]
    all_gather x0 -> x1, blocking collectives: none -> 7.15 us  [from_root(): return jnp.sum(lax.all_gather(block, axis), axis=0)]
  transfers between devices with their start and end apart: 2 -> 1, of which waited for: 2 -> 1; matrix products, arithmetic and copies ran while one was open for 1% -> 1% of each run, Pallas kernels for 0% -> 0%
where the time goes in v1:
time: 161 us
  waiting for transfers between devices  70.3 us (44%)
  local copies, waits for them, and re-layouts  28.8 us (18%)
  blocking collectives  28.7 us (18%)
  other arithmetic  14.9 us (9%)
  between operations  14.3 us (9%)
  matrix products  3.66 us (2%)
    psum x1, waiting for transfers between devices, per_device(): summed = lax.psum(partial_sums, ('row', 'col'))  70.3 us
    convert_element_type x1, local copies, waits for them, and re-layouts, per_device(): jnp.sum(local_slab.reshape(levels, third_rows, 3, third_cols, 3), axis=(2...  25.9 us
    all_gather x1, blocking collectives, per_device(): lax.all_gather(by_parent, 'row', axis=1, tiled=True)  15.1 us
    reduce_sum x1, other arithmetic, per_device(): jnp.sum(local_slab.reshape(levels, third_rows, 3, third_cols, 3), axis=(2...  11.8 us
    all_gather x1, blocking collectives, from_root(): return jnp.sum(lax.all_gather(block, axis), axis=0)  7.15 us
    all_gather x1, blocking collectives, per_device(): thirds = lax.all_gather(placed[:, :, None, :], 'grp', axis=2, tiled=True)  6.46 us
  transfers between devices with their start and end apart: 1, of which 1 were waited for; matrix products, arithmetic and copies ran while one was open for 1% of the time, Pallas kernels for 0%

profile of v1, /device:TPU:0, one launch (start us, length us, event | category | flops | bytes accessed | tf_op | source)
XLA Modules:
  0.0 160.7 jit_solution(10720829274543634851)
XLA Ops:
  6.5 0.7 select_reduce_fusion
  8.0 0.0 copy-start.1
  8.0 0.0 copy-start.3
  8.0 0.0 copy-start
  8.1 25.9 %reshape.136 = f32[4,16,3,256,3]{4,3,2,1,0:T(8,128)} reshape(bf16[1,4,48,768]{3,2,1,0:T(8,128)(2,1)} %param.5) | data formatting | bytes 884736 | tf_op jit(solution)/shard_map/convert_element_type | solution.py:62
  34.0 11.8 %reduce_sum.30 = f32[4,16,256]{2,1,0:T(8,128)S(1)} reduce(f32[4,16,3,256,3]{4,3,2,1,0:T(8,128)} %reshape.136, f32[]{:T(128)} %constant.140.clone.1), dimensions={2,4}, to_apply=%region_1.2 | reduce | flops 131072 | bytes 655364 | tf_op jit(solution)/shard_map/reduce_sum | solution.py:62
  45.8 0.5 gather_fusion
  46.3 0.1 broadcast_select_fusion.1
  46.4 15.1 %all_gather.12 = bf16[4,64,256]{2,1,0:T(8,128)(2,1)S(1)} all-gather(bf16[4,16,256]{2,1,0:T(8,128)(2,1)S(1)} %broadcast_select_fusion.1), channel_id=1, replica_groups=mesh['grp'=4,'row'=4,'col'=2] {'row'}, dimensions={1}, use_global_device_ids=true | all-gather | bytes 163840 | tf_op jit(solution)/shard_map/all_gather | solution.py:69
  61.5 0.1 copy.28
  61.6 0.7 gather_fusion.1
  62.3 0.1 fusion.24
  62.4 6.5 %all_gather.13 = bf16[4,48,4,256]{3,1,0,2:T(8,128)(2,1)S(1)} all-gather(bf16[4,48,1,256]{3,1,0,2:T(8,128)(2,1)S(1)} %fusion.24), channel_id=1, replica_groups=mesh['grp'=4,'row'=4,'col'=2] {'grp'}, dimensions={2}, use_global_device_ids=true | all-gather | bytes 491520 | tf_op jit(solution)/shard_map/all_gather | solution.py:71
  68.9 0.8 cosine_multiply_fusion.1
  69.7 0.3 fusion.21
  70.1 0.3 cosine_multiply_fusion.2
  70.4 0.1 fusion.40
  70.5 0.1 fusion.55
  70.6 0.3 fusion.13
  70.9 1.0 convolution_bitcast_fusion
  71.9 0.0 all-reduce.2.cloned.1.call-update
  71.9 0.3 fusion.20
  72.3 0.1 fusion.39
  72.4 0.6 gather_fusion.2
  73.0 0.1 copy.31
  73.1 70.3 %all-reduce.2.cloned.1.call-done = f32[4,64,64]{1,2,0:T(8,128)} async-done(((f32[4,64,64]{1,2,0:T(8,128)}), f32[4,64,64]{1,2,0:T(8,128)}) %all-reduce.2.cloned.1.call-update) | async-done | bytes 65552 | tf_op jit(solution)/shard_map/psum | solution.py:78
  143.5 0.1 copy.32
  143.6 7.1 %all-gather = f32[16,64,64]{2,1,0:T(8,128)S(1)} all-gather(f32[4,64,64]{2,1,0:T(8,128)S(1)} %copy.32), channel_id=2, replica_groups=mesh['grp'=4,'row'=4,'col'=2] {'grp'}, dimensions={0}, use_global_device_ids=true | all-gather | bytes 327680 | tf_op jit(solution)/shard_map/all_gather | solution.py:12
  150.8 0.1 copy.33
  150.9 0.6 gather_fusion.3
  151.5 0.9 fusion.5
  152.4 1.5 fusion.3
  (28 shorter events, 0.3 us)
Async XLA Ops:
  6.5 136.9 %all-reduce.2.cloned.1.call-start = ((), (), s32[]{:S(2)}) async-start(), calls=%async_computation | async-start | bytes 262144 | tf_op jit(solution)/shard_map/psum | solution.py:78
  8.0 62.6 %copy-start.1 = (bf16[1,4,48,768]{3,2,1,0:T(8,128)(2,1)S(1)}, bf16[1,4,48,768]{3,2,1,0:T(8,128)(2,1)}, u32[]{:S(2)}) copy-start(bf16[1,4,48,768]{3,2,1,0:T(8,128)(2,1)} %param.5) | copy-start | bytes 884740
  8.0 63.9 %copy-start.3 = (s32[4]{0:T(128)S(1)}, s32[4]{0:T(128)}, u32[]{:S(2)}) copy-start(s32[4]{0:T(128)} %param.7) | copy-start | bytes 52
  8.0 64.3 %copy-start = (f32[4]{0:T(128)S(1)}, f32[4]{0:T(128)}, u32[]{:S(2)}) copy-start(f32[4]{0:T(128)} %param.8) | copy-start | bytes 52
  8.0 65.0 %copy-start.2 = (f32[4,64,64]{2,1,0:T(8,128)S(1)}, f32[4,64,64]{2,1,0:T(8,128)}, u32[]{:S(2)}) copy-start(f32[4,64,64]{2,1,0:T(8,128)} %param.9) | copy-start | bytes 196612
Sparse Core Ops, SparseCore 0:
  72.0 71.4 all-reduce.1
